TPU v7x, 256 devices: a 2x2x32 block of a 4x8x32 slice. The times are simulated.
256 devices in a mesh: gp: 4 (over y, x), blk: 64 (over z, core).
Axes of the slice: x: 2, y: 2, z: 32, core: 2. Of those that a mesh axis runs over, the one named last changes fastest.
The devices are a block of a 4x8x32 slice.
Arguments:
- points: float32 [8, 65536], P(None, ('gp', 'blk')), parts along dimension 1, may hold values from -6 to 6
- vectors: float32 [8, 65536], P(None, ('gp', 'blk')), parts along dimension 1, may hold values from -6 to 6
- inv_length: float32 [32], P('gp'), parts along dimension 0, may hold values from 0.15 to 0.6
- noise: float32 [4], P('gp'), parts along dimension 0, may hold values from 0.1 to 1
Outputs:
- product: float32 [8, 65536], P(None, ('gp', 'blk')), parts along dimension 1
There are 4 independent parts, one for each index of `gp`. A program takes and returns all parts, laid end to end along the dimension named above; each array names one. Nothing has to cross between parts.
All inputs are finite; a program needn't handle non-finite values.
Results may differ from a plain program's by a relative error of at most 0.00017.
Values sent between devices are 32-bit elements; how exact they have to be, the bound alone decides.
A program may use at most 64 MiB of HBM per device.

v0:
```python
import jax
import jax.numpy as jnp
from jax import lax
from jax.sharding import PartitionSpec as P


def matern(left, right, inv_length):
    scaled_left = left * inv_length[:, None]
    scaled_right = right * inv_length[:, None]
    sq_left = jnp.sum(scaled_left * scaled_left, axis=0)
    sq_right = jnp.sum(scaled_right * scaled_right, axis=0)
    cross = jnp.dot(
        scaled_left.T,
        scaled_right,
        precision=lax.Precision.HIGHEST,
        preferred_element_type=jnp.float32,
    )
    dist2 = jnp.maximum(sq_left[:, None] + sq_right[None, :] - 2.0 * cross, 0.0)
    scaled_dist = jnp.sqrt(5.0 * dist2)
    return (1.0 + scaled_dist + scaled_dist * scaled_dist / 3.0) * jnp.exp(-scaled_dist)


def apply_tile(vec_other, tile):
    return jnp.dot(
        vec_other, tile, precision=lax.Precision.HIGHEST, preferred_element_type=jnp.float32
    )


def on_device(points, vectors, inv_length, noise):
    count = lax.axis_size("blk")
    total_points = points.shape[1] * count
    tile = matern(lax.all_gather(points, "blk", axis=1, tiled=True), points, inv_length)
    own_sum = apply_tile(lax.all_gather(vectors, "blk", axis=1, tiled=True), tile)
    return noise[0] * vectors + own_sum / jnp.sqrt(jnp.float32(total_points))


def solution(mesh):
    return jax.shard_map(
        on_device,
        mesh=mesh,
        in_specs=(P(None, ("gp", "blk")), P(None, ("gp", "blk")), P("gp"), P("gp")),
        out_specs=P(None, ("gp", "blk")),
        check_vma=False,
    )
```

profile of v0, /device:TPU:37, one launch (start us, length us, event | category | flops | bytes accessed | tf_op | source)
XLA Modules:
  0.0 170.3 jit_solution(1310754627161676833)
XLA Ops:
  0.0 0.0 copy-start
  0.0 78.1 %all_gather.6 = f32[8,16384]{1,0:T(8,128)S(1)} all-gather(f32[8,256]{1,0:T(8,128)} %param.4), channel_id=1, replica_groups=mesh['gp'=4,'blk'=64] {'blk'}, dimensions={1}, use_global_device_ids=true | all-gather | bytes 532480 | tf_op jit(solution)/shard_map/all_gather | solution.py:32
  78.1 0.9 multiply_reduce_fusion
  79.0 0.8 multiply_reduce_fusion.1
  79.8 23.7 %fusion.3 = f32[16384,256]{1,0:T(8,128)S(1)} fusion(f32[256]{0:T(256)S(1)} %multiply_reduce_fusion.1, f32[16384]{0:T(1024)S(1)} %multiply_reduce_fusion, f32[8,16384]{1,0:T(8,128)S(1)} %all_gather.6, f32[8]{0:T(128)} %param.6, f32[8,256]{1,0:T(8,128)} %param.4), kind=kOutput, calls=%fused_computation.4 | convolution fusion | flops 423757824 | bytes 17376288 | tf_op jit(solution)/shard_map/dot_general | solution.py:12
  103.5 0.0 copy-done
  103.5 54.1 %all_gather.7 = f32[8,16384]{1,0:T(8,128)S(1)} all-gather(f32[8,256]{1,0:T(8,128)S(1)} %copy-done), channel_id=1, replica_groups=mesh['gp'=4,'blk'=64] {'blk'}, dimensions={1}, use_global_device_ids=true | all-gather | bytes 532480 | tf_op jit(solution)/shard_map/all_gather | solution.py:33
  158.2 12.1 %fusion.20 = f32[8,256]{1,0:T(8,128)} fusion(f32[8,16384]{1,0:T(8,128)S(1)} %all_gather.7, f32[16384,256]{1,0:T(8,128)S(1)} %fusion.3, f32[8,256]{1,0:T(8,128)S(1)} %copy-done, f32[]{:T(128)} %bitcast.6), kind=kOutput, calls=%fused_computation.17 | convolution fusion | flops 427825152 | bytes 17317892 | tf_op jit(solution)/shard_map/dot_general | solution.py:24
Async XLA Ops:
  0.0 103.5 %copy-start = (f32[8,256]{1,0:T(8,128)S(1)}, f32[8,256]{1,0:T(8,128)}, u32[]{:S(2)}) copy-start(f32[8,256]{1,0:T(8,128)} %param.5) | copy-start | bytes 24580
where the time goes:
time: 171 us; the launch traced here: 170 us
  blocking collectives  132 us (77%)
  matrix products  35.8 us (21%)
    all_gather x1, blocking collectives, on_device(): lax.all_gather(points, 'blk', axis=1, tiled=True)  78.1 us
    all_gather x1, blocking collectives, on_device(): lax.all_gather(vectors, 'blk', axis=1, tiled=True)  54.1 us
    dot_general x1, matrix products, matern(): jnp.dot(scaled_left.T, scaled_right, precision=lax.Precision.HIGHEST, pre...  23.7 us
    dot_general x1, matrix products, apply_tile(): jnp.dot(vec_other, tile, precision=lax.Precision.HIGHEST, preferred_eleme...  12.1 us

commit v1 on v0

--- a/solution.py
+++ b/solution.py
@@ -2,6 +2,14 @@
 import jax.numpy as jnp
 from jax import lax
 from jax.sharding import PartitionSpec as P
+
+
+def tiled_gather(shard, axis, dim):
+    size = lax.axis_size(axis)
+    repeats = [size if d == dim else 1 for d in range(shard.ndim)]
+    return lax.all_to_all(
+        jnp.tile(shard, repeats), axis, split_axis=dim, concat_axis=dim, tiled=True
+    )
 
 
 def matern(left, right, inv_length):
@@ -29,7 +37,7 @@
 def on_device(points, vectors, inv_length, noise):
     count = lax.axis_size("blk")
     total_points = points.shape[1] * count
-    tile = matern(lax.all_gather(points, "blk", axis=1, tiled=True), points, inv_length)
+    tile = matern(tiled_gather(points, "blk", 1), points, inv_length)
     own_sum = apply_tile(lax.all_gather(vectors, "blk", axis=1, tiled=True), tile)
     return noise[0] * vectors + own_sum / jnp.sqrt(jnp.float32(total_points))
 

time: 171 us -> 173 us (1.012)
  starting transfers between devices: 0 us -> 34.3 us
  blocking collectives: 132 us -> 97.8 us
    all_gather x1 -> x0, blocking collectives: 78.1 us -> none  [on_device(): lax.all_gather(points, 'blk', axis=1, tiled=True)]
    all_gather x1, blocking collectives: 54.1 us -> 97.8 us  [on_device(): lax.all_gather(vectors, 'blk', axis=1, tiled=True)]
    all_to_all x0 -> x1, starting transfers between devices: none -> 34.3 us  [tiled_gather(): lax.all_to_all(jnp.tile(shard, repeats), axis, split_axis=dim, concat_axi...]
  transfers between devices with their start and end apart: 0 -> 1, of which waited for: 0 -> 0; matrix products, arithmetic and copies ran while one was open for 0% -> 0% of each run, Pallas kernels for 0% -> 0%
where the time goes in v1:
time: 173 us; the launch traced here: 172 us
  blocking collectives  97.8 us (57%)
  matrix products  36.1 us (21%)
  starting transfers between devices  34.3 us (20%)
    all_gather x1, blocking collectives, on_device(): lax.all_gather(vectors, 'blk', axis=1, tiled=True)  97.8 us
    all_to_all x1, starting transfers between devices, tiled_gather(): lax.all_to_all(jnp.tile(shard, repeats), axis, split_axis=dim, concat_axi...  34.3 us
    dot_general x1, matrix products, matern(): jnp.dot(scaled_left.T, scaled_right, precision=lax.Precision.HIGHEST, pre...  24 us
    dot_general x1, matrix products, apply_tile(): jnp.dot(vec_other, tile, precision=lax.Precision.HIGHEST, preferred_eleme...  12.1 us
  transfers between devices with their start and end apart: 1, of which 0 were waited for; matrix products, arithmetic and copies ran while one was open for 0% of the time, Pallas kernels for 0%

profile of v1, /device:TPU:37, one launch (start us, length us, event | category | flops | bytes accessed | tf_op | source)
XLA Modules:
  0.0 172.2 jit_solution(3347644368773600278)
XLA Ops:
  0.0 0.0 copy-start
  0.0 1.5 tile.2
  1.5 34.3 %all-to-all-start = ((f32[8,64,256]{2,0,1:T(8,128)}), f32[8,64,256]{2,0,1:T(8,128)S(1)}, u32[]{:S(2)}, u32[]{:S(2)}) async-start(f32[8,64,256]{2,0,1:T(8,128)} %tile.2), calls=%async_computation | async-start | bytes 1048576 | tf_op jit(solution)/shard_map/all_to_all | solution.py:10
  36.5 0.8 multiply_reduce_fusion.1
  37.3 97.8 %all_gather.3 = f32[8,16384]{1,0:T(8,128)S(1)} all-gather(f32[8,256]{1,0:T(8,128)} %param.5), channel_id=1, replica_groups=mesh['gp'=4,'blk'=64] {'blk'}, dimensions={1}, use_global_device_ids=true | all-gather | bytes 532480 | tf_op jit(solution)/shard_map/all_gather | solution.py:41
  135.1 0.0 all-to-all-done
  135.1 0.9 multiply_reduce_fusion
  136.1 24.0 %fusion.3 = f32[16384,256]{1,0:T(8,128)S(1)} fusion(f32[256]{0:T(256)S(1)} %multiply_reduce_fusion.1, f32[16384]{0:T(1024)S(1)} %bitcast.12, f32[8,16384]{1,0:T(8,128)S(1)} %bitcast.10, f32[8]{0:T(128)} %param.6, f32[8,256]{1,0:T(8,128)} %param.4), kind=kOutput, calls=%fused_computation.4 | convolution fusion | flops 423757824 | bytes 17376288 | tf_op jit(solution)/shard_map/dot_general | solution.py:20
  160.1 0.0 copy-done
  160.1 12.1 %fusion.20 = f32[8,256]{1,0:T(8,128)} fusion(f32[8,16384]{1,0:T(8,128)S(1)} %all_gather.3, f32[16384,256]{1,0:T(8,128)S(1)} %fusion.3, f32[8,256]{1,0:T(8,128)S(1)} %copy-done, f32[]{:T(128)} %bitcast.9), kind=kOutput, calls=%fused_computation.17 | convolution fusion | flops 427825152 | bytes 17317892 | tf_op jit(solution)/shard_map/dot_general | solution.py:32
  (1 shorter events, 0.0 us)
Async XLA Ops:
  0.0 160.1 %copy-start = (f32[8,256]{1,0:T(8,128)S(1)}, f32[8,256]{1,0:T(8,128)}, u32[]{:S(2)}) copy-start(f32[8,256]{1,0:T(8,128)} %param.5) | copy-start | bytes 24580
  1.5 133.6 %all-to-all-start = ((f32[8,64,256]{2,0,1:T(8,128)}), f32[8,64,256]{2,0,1:T(8,128)S(1)}, u32[]{:S(2)}, u32[]{:S(2)}) async-start(f32[8,64,256]{2,0,1:T(8,128)} %tile.2), calls=%async_computation | async-start | bytes 1048576 | tf_op jit(solution)/shard_map/all_to_all | solution.py:10
